TPU v7x, 32 devices: a whole 2x2x4 slice. The times are simulated.
32 devices in a mesh: pipe: 4 (over z), row: 4 (over x, core), col: 2 (over y).
Axes of the slice: x: 2, y: 2, z: 4, core: 2. Of those that a mesh axis runs over, the one named last changes fastest.
Arguments:
- weights: bfloat16 [4, 4096, 14336], P('pipe', 'col', 'row'), may hold values from -0.09375 to 0.09375
- fwd_resid: bfloat16 [4, 128, 4096], P('pipe', None, 'col'), may hold values from -6 to 6
- fwd_hidden: bfloat16 [4, 128, 14336], P('pipe', None, 'row'), may hold values from -6 to 6
- bwd_resid: bfloat16 [4, 128, 4096], P('pipe', None, 'col'), may hold values from -6 to 6
- bwd_hidden: bfloat16 [4, 128, 14336], P('pipe', None, 'row'), may hold values from -6 to 6
- saved_pre: bfloat16 [4, 4, 128, 14336], P(None, 'pipe', None, 'row'), may hold values from -6 to 6
- pool_embed: bfloat16 [3, 128, 4096], P(None, None, 'col'), may hold values from -6 to 6
- pool_mask: int32 [3, 128], replicated, may hold values 0 or 1
- pool_stratum: int32 [3], replicated, may hold values from 0 to 7
- order: int32 [3], replicated, may hold values from 0 to 2, each once
- mask_vec: bfloat16 [4096], P('col'), may hold values from -6 to 6
- ratio_table: bfloat16 [8, 4096], P(None, 'col'), may hold values from -6 to 6
- cot_inject: bfloat16 [3, 128, 4096], P(None, None, 'col'), may hold values from -6 to 6
Outputs:
- out_resid: bfloat16 [2, 4, 128, 4096], P(None, 'pipe', None, 'col')
- out_hidden: bfloat16 [4, 128, 14336], P('pipe', 'col', 'row')
Inputs may be any that keep to these rules, and one draw needn't show every extreme that they name: `order`: each waiting micro-batch enters exactly once.
All inputs are finite; a program needn't handle non-finite values.
Results may differ from a plain program's by a relative error of at most 0.025.
Values may be sent and summed in bfloat16 or wider, within the bound.
No kernel may reach another device: no remote copies, remote signals or barrier semaphores. Data moves between devices by JAX's collectives and lax.ppermute only.
A program may use at most 64 MiB of HBM per device.

v0:
```python
import jax
import jax.numpy as jnp
from jax import lax
from jax.sharding import PartitionSpec as P

STEPS = 4


def extended_2(shard, sides, width):
    for axis, dim in sides:
        size, length = (lax.axis_size(axis), shard.shape[dim])
        up = [(i, (i + 1) % size) for i in range(size - 1)]
        down = [(j, i) for i, j in up]
        last = lax.slice_in_dim(shard, length - width, length, axis=dim)
        first = lax.slice_in_dim(shard, 0, width, axis=dim)
        before = lax.ppermute(last, axis, up)
        after = lax.ppermute(first, axis, down)
        shard = jnp.concatenate([before, shard, after], axis=dim)
    return shard


def swapped(value, axis, stride):
    mask = 2**stride
    pairs = [(source, source ^ mask) for source in range(lax.axis_size(axis))]
    return lax.ppermute(value, axis, pairs)


def silu_grad(preact):
    sigma = jax.nn.sigmoid(preact)
    return sigma * (1.0 + preact * (1.0 - sigma))


def inject(step_idx, pool_embed, pool_mask, pool_stratum, order, mask_vec, ratio_table):
    chosen = order[step_idx - 1]
    embedded = pool_embed[chosen]
    masked = pool_mask[chosen]
    stratum = pool_stratum[chosen]
    onehot = (jnp.arange(ratio_table.shape[0], dtype=jnp.int32) == stratum).astype(jnp.bfloat16)
    condition = jnp.dot(onehot, ratio_table, preferred_element_type=jnp.float32)
    chosen_rows = jnp.where(
        masked[:, None] == 1, mask_vec[None, :].astype(jnp.float32), embedded.astype(jnp.float32)
    )
    return (chosen_rows + condition[None, :]).astype(jnp.bfloat16)


def shards(
    weights,
    fwd_resid,
    fwd_hidden,
    bwd_resid,
    bwd_hidden,
    saved_pre,
    pool_embed,
    pool_mask,
    pool_stratum,
    order,
    mask_vec,
    ratio_table,
    cot_inject,
):
    weight = weights[0]
    fwd_res = fwd_resid[0]
    fwd_hid = fwd_hidden[0]
    bwd_res = bwd_resid[0]
    bwd_hid = bwd_hidden[0]
    position = lax.axis_index("pipe")
    sections = lax.axis_size("pipe")
    is_even = position % 2 == 0
    token_rows = fwd_res.shape[0]
    col_rows = token_rows // lax.axis_size("col")
    fwd_out, bwd_out, hid_share = (fwd_res, bwd_res, fwd_hid)
    for step_idx in range(STEPS):
        operand = jnp.where(is_even, fwd_res, bwd_res)

        def feature_term(offset, length, operand=operand):
            return jnp.dot(operand, weight, preferred_element_type=jnp.float32)

        preact = lax.psum_scatter(
            feature_term(jnp.int32(0), col_rows * lax.axis_size("col")).astype(jnp.bfloat16),
            "col",
            scatter_dimension=0,
            tiled=True,
        ).astype(jnp.float32)
        hid_share = jnp.where(is_even, jax.nn.silu(preact), preact).astype(jnp.bfloat16)
        hid_grad = (
            bwd_hid.astype(jnp.float32) * silu_grad(saved_pre[step_idx, 0].astype(jnp.float32))
        ).astype(jnp.bfloat16)
        hid_operand = jnp.where(is_even, hid_grad, fwd_hid)
        residual = jnp.where(is_even, bwd_res, fwd_res)
        product = lax.dot_general(
            hid_operand, weight, (((1,), (1,)), ((), ())), preferred_element_type=jnp.float32
        )
        updated = (
            residual.astype(jnp.float32)
            + lax.psum(product.astype(jnp.bfloat16), "row").astype(jnp.float32)
        ).astype(jnp.bfloat16)
        fwd_out = jnp.where(is_even, fwd_res, updated)
        bwd_out = jnp.where(is_even, updated, bwd_res)
        if step_idx + 1 < STEPS:
            hid_send = lax.all_gather(hid_share, "col", axis=0, tiled=True)
            res_rows = fwd_out.size // 128
            buffer = jnp.concatenate(
                [bwd_out.reshape(res_rows, 128), fwd_out.reshape(res_rows, 128)], 0
            )
            extended = extended_2(buffer, (("pipe", 0),), res_rows)
            left_resid = extended[:res_rows]
            right_resid = extended[extended.shape[0] - res_rows :]
            partner_hidden = swapped(hid_send, "pipe", 0)
            fwd_hid = partner_hidden
            bwd_hid = partner_hidden
            incoming = inject(
                step_idx + 1, pool_embed, pool_mask, pool_stratum, order, mask_vec, ratio_table
            )
            fwd_res = jnp.where(position == 0, incoming, left_resid.reshape(fwd_out.shape))
            bwd_res = jnp.where(
                position == sections - 1, cot_inject[step_idx], right_resid.reshape(bwd_out.shape)
            )
    out_resid = jnp.stack([fwd_out, bwd_out])[:, None]
    return (out_resid, hid_share[None])


def solution(mesh):
    return jax.shard_map(
        shards,
        mesh=mesh,
        in_specs=(
            P("pipe", "col", "row"),
            P("pipe", None, "col"),
            P("pipe", None, "row"),
            P("pipe", None, "col"),
            P("pipe", None, "row"),
            P(None, "pipe", None, "row"),
            P(None, None, "col"),
            P(),
            P(),
            P(),
            P("col"),
            P(None, "col"),
            P(None, None, "col"),
        ),
        out_specs=(P(None, "pipe", None, "col"), P("pipe", "col", "row")),
        check_vma=False,
    )
```

profile of v0, /device:TPU:0, one launch (start us, length us, event | category | flops | bytes accessed | tf_op | source)
XLA Modules:
  0.0 378.4 jit_solution(14535607205255028792)
XLA Ops:
  7.2 8.4 %fusion.16 = bf16[128,3584]{1,0:T(8,128)(2,1)} fusion(bf16[1,2048,3584]{2,1,0:T(8,128)(2,1)} %param.13, bf16[1,128,2048]{2,1,0:T(8,128)(2,1)} %param.14, bf16[1,128,2048]{2,1,0:T(8,128)(2,1)} %param.16, pred[]{:T(512)S(6)} %eq.66), kind=kOutput, calls=%fused_computation.16 | convolution fusion | flops 1879769088 | bytes 16646145 | tf_op jit(solution)/shard_map/dot_general | solution.py:76
  15.7 21.8 %reduce-scatter.5.cloned.1.call-done = bf16[64,3584]{1,0:T(8,128)(2,1)} async-done(((bf16[128,3584]{1,0:T(8,128)(2,1)}), bf16[64,3584]{1,0:T(8,128)(2,1)}) %reduce-scatter.5.cloned.1.call-update) | async-done | bytes 458768 | tf_op jit(solution)/shard_map/reduce_scatter | solution.py:78
  38.8 12.7 %all_gather.9 = bf16[128,3584]{1,0:T(8,128)(2,1)S(1)} all-gather(bf16[64,3584]{1,0:T(8,128)(2,1)S(1)} %fusion.98), channel_id=1, replica_groups=mesh['pipe'=4,'row'=4,'col'=2] {'col'}, dimensions={0}, use_global_device_ids=true | all-gather | bytes 1376256 | tf_op jit(solution)/shard_map/all_gather | solution.py:100
  53.0 11.1 %fusion.28 = bf16[128,2048]{1,0:T(8,128)(2,1)} fusion(bf16[1,2048,3584]{2,1,0:T(8,128)(2,1)} %param.13, bf16[1,128,3584]{2,1,0:T(8,128)(2,1)S(1)} %copy-done.8, bf16[1,128,3584]{2,1,0:T(8,128)(2,1)S(1)} %copy-done.9, bf16[4,1,128,3584]{3,2,1,0:T(8,128)(2,1)} %param.18, pred[]{:T(512)S(6)} %eq.66), kind=kOutput, calls=%fused_computation.20 | convolution fusion | flops 1884815360 | bytes 17956864 | tf_op jit(solution)/shard_map/dot_general | solution.py:90
  64.1 8.4 %collective-permute-done.2 = bf16[128,3584]{1,0:T(8,128)(2,1)S(1)} collective-permute-done((bf16[128,3584]{1,0:T(8,128)(2,1)S(1)}, bf16[128,3584]{1,0:T(8,128)(2,1)S(1)}, u32[]{:S(2)}, u32[]{:S(2)}) %collective-permute-start.2) | collective-permute-done | bytes 917536 | tf_op jit(solution)/shard_map/ppermute | solution.py:25
  72.6 11.1 %fusion.31 = bf16[128,2048]{1,0:T(8,128)(2,1)} fusion(bf16[1,2048,3584]{2,1,0:T(8,128)(2,1)} %param.13, bf16[128,3584]{1,0:T(8,128)(2,1)S(1)} %collective-permute-done.2, bf16[4,1,128,3584]{3,2,1,0:T(8,128)(2,1)} %param.18, pred[]{:T(512)S(6)} %eq.66), kind=kOutput, calls=%fused_computation.21 | convolution fusion | flops 1884815360 | bytes 17039360 | tf_op jit(solution)/shard_map/dot_general | solution.py:90
  92.0 28.2 %all-reduce.7.cloned.1.call-done = (bf16[128,2048]{1,0:T(8,128)(2,1)}, bf16[128,2048]{1,0:T(8,128)(2,1)}) async-done(((bf16[128,2048]{1,0:T(8,128)(2,1)}, bf16[128,2048]{1,0:T(8,128)(2,1)}), (bf16[128,2048]{1,0:T(8,128)(2,1)}, bf16[128,2048]{1,0:T(8,128)(2,1)})) %all-reduce.7.cloned.1.call-update) | async-done | bytes 1048592 | tf_op jit(solution)/shard_map/psum | solution.py:95
  120.2 2.5 bitcast_select_fusion.11
  124.9 4.2 %collective-permute-start = (bf16[2048,128]{1,0:T(8,128)(2,1)}, bf16[2048,128]{1,0:T(8,128)(2,1)}, u32[]{:S(2)}, u32[]{:S(2)}) collective-permute-start(bf16[2048,128]{1,0:T(8,128)(2,1)} %reshape.152), channel_id=1, source_target_pairs={{0,8},{8,16},{16,24},{1,9},{9,17},{17,25},{2,10},{10,18},{18,26},{... | collective-permute-start | bytes 1572872 | tf_op jit(solution)/shard_map/ppermute | solution.py:16
  134.0 2.5 reshape.171
  141.2 4.9 %collective-permute-done.1 = bf16[2048,128]{1,0:T(8,128)(2,1)} collective-permute-done((bf16[2048,128]{1,0:T(8,128)(2,1)}, bf16[2048,128]{1,0:T(8,128)(2,1)}, u32[]{:S(2)}, u32[]{:S(2)}) %collective-permute-start.1) | collective-permute-done | bytes 524320 | tf_op jit(solution)/shard_map/ppermute | solution.py:17
  148.2 2.8 broadcast_select_fusion.2
  153.0 3.6 collective-permute-start.3
  166.2 6.4 %collective-permute-done.4 = bf16[2048,128]{1,0:T(8,128)(2,1)} collective-permute-done((bf16[2048,128]{1,0:T(8,128)(2,1)}, bf16[2048,128]{1,0:T(8,128)(2,1)}, u32[]{:S(2)}, u32[]{:S(2)}) %collective-permute-start.4) | collective-permute-done | bytes 524320 | tf_op jit(solution)/shard_map/ppermute | solution.py:17
  172.6 3.0 fusion.128
  177.7 8.4 %fusion.19 = bf16[128,3584]{1,0:T(8,128)(2,1)} fusion(bf16[128,2048]{1,0:T(8,128)(2,1)} %select_n.258, bf16[1,2048,3584]{2,1,0:T(8,128)(2,1)} %param.13), kind=kOutput, calls=%fused_computation.17 | convolution fusion | flops 1879506944 | bytes 16121856 | tf_op jit(solution)/shard_map/dot_general | solution.py:76
  188.2 8.7 %fusion.22 = bf16[128,3584]{1,0:T(8,128)(2,1)} fusion(bf16[128,2048]{1,0:T(8,128)(2,1)} %select_n.270, bf16[1,2048,3584]{2,1,0:T(8,128)(2,1)} %param.13), kind=kOutput, calls=%fused_computation.18 | convolution fusion | flops 1879506944 | bytes 16121856 | tf_op jit(solution)/shard_map/dot_general | solution.py:76
  196.9 7.1 %reduce-scatter.7.cloned.1.call-done = bf16[64,3584]{1,0:T(8,128)(2,1)} async-done(((bf16[128,3584]{1,0:T(8,128)(2,1)}), bf16[64,3584]{1,0:T(8,128)(2,1)}) %reduce-scatter.7.cloned.1.call-update) | async-done | bytes 458768 | tf_op jit(solution)/shard_map/reduce_scatter | solution.py:78
  205.3 18.1 %all_gather.10 = bf16[128,3584]{1,0:T(8,128)(2,1)} all-gather(bf16[64,3584]{1,0:T(8,128)(2,1)S(1)} %fusion.99), channel_id=1, replica_groups=mesh['pipe'=4,'row'=4,'col'=2] {'col'}, dimensions={0}, use_global_device_ids=true | all-gather | bytes 1376256 | tf_op jit(solution)/shard_map/all_gather | solution.py:100
  224.9 4.2 %reduce-scatter.9.cloned.1.call-done = bf16[64,3584]{1,0:T(8,128)(2,1)} async-done(((bf16[128,3584]{1,0:T(8,128)(2,1)}), bf16[64,3584]{1,0:T(8,128)(2,1)}) %reduce-scatter.9.cloned.1.call-update) | async-done | bytes 458768 | tf_op jit(solution)/shard_map/reduce_scatter | solution.py:78
  230.4 13.0 %all_gather.11 = bf16[128,3584]{1,0:T(8,128)(2,1)S(1)} all-gather(bf16[64,3584]{1,0:T(8,128)(2,1)S(1)} %fusion.100), channel_id=1, replica_groups=mesh['pipe'=4,'row'=4,'col'=2] {'col'}, dimensions={0}, use_global_device_ids=true | all-gather | bytes 1376256 | tf_op jit(solution)/shard_map/all_gather | solution.py:100
  244.9 11.7 %fusion.34 = bf16[128,2048]{1,0:T(8,128)(2,1)} fusion(bf16[1,2048,3584]{2,1,0:T(8,128)(2,1)} %param.13, bf16[128,3584]{1,0:T(8,128)(2,1)} %collective-permute-done.5, bf16[4,1,128,3584]{3,2,1,0:T(8,128)(2,1)} %param.18, pred[]{:T(512)S(6)} %eq.66), kind=kOutput, calls=%fused_computation.22 | convolution fusion | flops 1884815360 | bytes 17039360 | tf_op jit(solution)/shard_map/dot_general | solution.py:90
  256.5 8.2 %collective-permute-done.8 = bf16[128,3584]{1,0:T(8,128)(2,1)S(1)} collective-permute-done((bf16[128,3584]{1,0:T(8,128)(2,1)S(1)}, bf16[128,3584]{1,0:T(8,128)(2,1)S(1)}, u32[]{:S(2)}, u32[]{:S(2)}) %collective-permute-start.8) | collective-permute-done | bytes 917536 | tf_op jit(solution)/shard_map/ppermute | solution.py:25
  264.8 11.0 %fusion.37 = bf16[128,2048]{1,0:T(8,128)(2,1)} fusion(bf16[1,2048,3584]{2,1,0:T(8,128)(2,1)} %param.13, bf16[128,3584]{1,0:T(8,128)(2,1)S(1)} %collective-permute-done.8, bf16[4,1,128,3584]{3,2,1,0:T(8,128)(2,1)} %param.18, pred[]{:T(512)S(6)} %eq.66), kind=kOutput, calls=%fused_computation.23 | convolution fusion | flops 1884815360 | bytes 17039360 | tf_op jit(solution)/shard_map/dot_general | solution.py:90
  280.2 32.1 %all-reduce.5.cloned.1.call-done = (bf16[128,2048]{1,0:T(8,128)(2,1)}, bf16[128,2048]{1,0:T(8,128)(2,1)}) async-done(((bf16[128,2048]{1,0:T(8,128)(2,1)}, bf16[128,2048]{1,0:T(8,128)(2,1)}), (bf16[128,2048]{1,0:T(8,128)(2,1)}, bf16[128,2048]{1,0:T(8,128)(2,1)})) %all-reduce.5.cloned.1.call-update) | async-done | bytes 1048592 | tf_op jit(solution)/shard_map/psum | solution.py:95
  312.3 2.8 broadcast_select_fusion.1
  317.1 4.3 %collective-permute-start.6 = (bf16[2048,128]{1,0:T(8,128)(2,1)}, bf16[2048,128]{1,0:T(8,128)(2,1)}, u32[]{:S(2)}, u32[]{:S(2)}) collective-permute-start(bf16[2048,128]{1,0:T(8,128)(2,1)} %reshape.160), channel_id=1, source_target_pairs={{0,8},{8,16},{16,24},{1,9},{9,17},{17,25},{2,10},{10,18},{18,26},{... | collective-permute-start | bytes 1572872 | tf_op jit(solution)/shard_map/ppermute | solution.py:16
  325.0 2.4 reshape.173
  331.6 7.0 %collective-permute-done.7 = bf16[2048,128]{1,0:T(8,128)(2,1)} collective-permute-done((bf16[2048,128]{1,0:T(8,128)(2,1)}, bf16[2048,128]{1,0:T(8,128)(2,1)}, u32[]{:S(2)}, u32[]{:S(2)}) %collective-permute-start.7) | collective-permute-done | bytes 524320 | tf_op jit(solution)/shard_map/ppermute | solution.py:17
  338.6 2.3 fusion.124
  342.9 8.4 %fusion.25 = bf16[128,3584]{1,0:T(8,128)(2,1)} fusion(bf16[128,2048]{1,0:T(8,128)(2,1)} %select_n.279, bf16[1,2048,3584]{2,1,0:T(8,128)(2,1)} %param.13), kind=kOutput, calls=%fused_computation.19 | convolution fusion | flops 1879506944 | bytes 16121856 | tf_op jit(solution)/shard_map/dot_general | solution.py:76
  358.3 11.2 %reduce-scatter.11.cloned.1.call-done = bf16[64,3584]{1,0:T(8,128)(2,1)} async-done(((bf16[128,3584]{1,0:T(8,128)(2,1)}), bf16[64,3584]{1,0:T(8,128)(2,1)}) %reduce-scatter.11.cloned.1.call-update) | async-done | bytes 458768 | tf_op jit(solution)/shard_map/reduce_scatter | solution.py:78
  (82 shorter events, 66.0 us)
Async XLA Ops:
  7.2 130.0 %copy-start = (bf16[8,2048]{1,0:T(8,128)(2,1)S(1)}, bf16[8,2048]{1,0:T(8,128)(2,1)}, u32[]{:S(2)}) copy-start(bf16[8,2048]{1,0:T(8,128)(2,1)} %param.24) | copy-start | bytes 98308
  7.2 30.3 %reduce-scatter.5.cloned.1.call-start = ((), (), s32[]{:S(2)}) async-start(), calls=%async_computation.4 | async-start | bytes 1376256 | tf_op jit(solution)/shard_map/reduce_scatter | solution.py:78
  15.6 37.4 %copy-start.8 = (bf16[1,128,3584]{2,1,0:T(8,128)(2,1)S(1)}, bf16[1,128,3584]{2,1,0:T(8,128)(2,1)}, u32[]{:S(2)}) copy-start(bf16[1,128,3584]{2,1,0:T(8,128)(2,1)} %param.15) | copy-start | bytes 2752516
  15.6 37.4 %copy-start.9 = (bf16[1,128,3584]{2,1,0:T(8,128)(2,1)S(1)}, bf16[1,128,3584]{2,1,0:T(8,128)(2,1)}, u32[]{:S(2)}) copy-start(bf16[1,128,3584]{2,1,0:T(8,128)(2,1)} %param.17) | copy-start | bytes 2752516
  15.6 104.6 %all-reduce.7.cloned.1.call-start = ((), (), s32[]{:S(2)}) async-start(), calls=%async_computation.9 | async-start | bytes 2097152 | tf_op jit(solution)/shard_map/psum | solution.py:95
  51.5 21.0 %collective-permute-start.2 = (bf16[128,3584]{1,0:T(8,128)(2,1)S(1)}, bf16[128,3584]{1,0:T(8,128)(2,1)S(1)}, u32[]{:S(2)}, u32[]{:S(2)}) collective-permute-start(bf16[128,3584]{1,0:T(8,128)(2,1)S(1)} %all_gather.9), channel_id=1, source_target_pairs={{0,8},{8,0},{16,24},{24,16},{1,9},{9,1},{17,25},{25,17},{2,10},{10... | collective-permute-start | bytes 2752520 | tf_op jit(solution)/shard_map/ppermute | solution.py:25
  64.1 19.6 %copy-start.4 = (s32[3]{0:T(128)S(1)}, s32[3]{0:T(128)}, u32[]{:S(2)}) copy-start(s32[3]{0:T(128)} %param.22) | copy-start | bytes 40
  72.5 17.7 %copy-start.1 = (bf16[3,128,2048]{2,1,0:T(8,128)(2,1)S(1)}, bf16[3,128,2048]{2,1,0:T(8,128)(2,1)}, u32[]{:S(2)}) copy-start(bf16[3,128,2048]{2,1,0:T(8,128)(2,1)} %param.19) | copy-start | bytes 4718596
  83.7 120.3 %reduce-scatter.7.cloned.1.call-start = ((), (), s32[]{:S(2)}) async-start(), calls=%async_computation.5 | async-start | bytes 1376256 | tf_op jit(solution)/shard_map/reduce_scatter | solution.py:78
  90.2 30.0 %copy-start.3 = (bf16[1,128,2048]{2,1,0:T(8,128)(2,1)S(1)}, bf16[1,128,2048]{2,1,0:T(8,128)(2,1)}, u32[]{:S(2)}) copy-start(bf16[1,128,2048]{2,1,0:T(8,128)(2,1)} %param.14) | copy-start | bytes 1572868
  120.2 12.2 %copy-start.7 = (s32[3,128]{1,0:T(4,128)S(1)}, s32[3,128]{1,0:T(4,128)}, u32[]{:S(2)}) copy-start(s32[3,128]{1,0:T(4,128)} %param.20) | copy-start | bytes 4612
  124.9 14.3 %collective-permute-start = (bf16[2048,128]{1,0:T(8,128)(2,1)}, bf16[2048,128]{1,0:T(8,128)(2,1)}, u32[]{:S(2)}, u32[]{:S(2)}) collective-permute-start(bf16[2048,128]{1,0:T(8,128)(2,1)} %reshape.152), channel_id=1, source_target_pairs={{0,8},{8,16},{16,24},{1,9},{9,17},{17,25},{2,10},{10,18},{18,26},{... | collective-permute-start | bytes 1572872 | tf_op jit(solution)/shard_map/ppermute | solution.py:16
  131.1 15.0 %collective-permute-start.1 = (bf16[2048,128]{1,0:T(8,128)(2,1)}, bf16[2048,128]{1,0:T(8,128)(2,1)}, u32[]{:S(2)}, u32[]{:S(2)}) collective-permute-start(bf16[2048,128]{1,0:T(8,128)(2,1)} %reshape.154), channel_id=1, source_target_pairs={{8,0},{16,8},{24,16},{9,1},{17,9},{25,17},{10,2},{18,10},{26,18},{... | collective-permute-start | bytes 1572872 | tf_op jit(solution)/shard_map/ppermute | solution.py:17
  132.8 3.7 copy-start.5
  132.8 4.3 %copy-start.6 = (bf16[2048]{0:T(1024)(128)(2,1)S(1)}, bf16[2048]{0:T(1024)(128)(2,1)}, u32[]{:S(2)}) copy-start(bf16[2048]{0:T(1024)(128)(2,1)} %param.23) | copy-start | bytes 12292
  134.0 14.2 %copy-start.2 = (bf16[3,128,2048]{2,1,0:T(8,128)(2,1)S(1)}, bf16[3,128,2048]{2,1,0:T(8,128)(2,1)}, u32[]{:S(2)}) copy-start(bf16[3,128,2048]{2,1,0:T(8,128)(2,1)} %param.25) | copy-start | bytes 4718596
  153.0 13.2 %collective-permute-start.3 = (bf16[2048,128]{1,0:T(8,128)(2,1)}, bf16[2048,128]{1,0:T(8,128)(2,1)}, u32[]{:S(2)}, u32[]{:S(2)}) collective-permute-start(bf16[2048,128]{1,0:T(8,128)(2,1)} %reshape.156), channel_id=1, source_target_pairs={{0,8},{8,16},{16,24},{1,9},{9,17},{17,25},{2,10},{10,18},{18,26},{... | collective-permute-start | bytes 1572872 | tf_op jit(solution)/shard_map/ppermute | solution.py:16
  158.7 13.9 %collective-permute-start.4 = (bf16[2048,128]{1,0:T(8,128)(2,1)}, bf16[2048,128]{1,0:T(8,128)(2,1)}, u32[]{:S(2)}, u32[]{:S(2)}) collective-permute-start(bf16[2048,128]{1,0:T(8,128)(2,1)} %reshape.158), channel_id=1, source_target_pairs={{8,0},{16,8},{24,16},{9,1},{17,9},{25,17},{10,2},{18,10},{26,18},{... | collective-permute-start | bytes 1572872 | tf_op jit(solution)/shard_map/ppermute | solution.py:17
  186.1 43.0 %reduce-scatter.9.cloned.1.call-start = ((), (), s32[]{:S(2)}) async-start(), calls=%async_computation.6 | async-start | bytes 1376256 | tf_op jit(solution)/shard_map/reduce_scatter | solution.py:78
  196.9 115.4 %all-reduce.5.cloned.1.call-start = ((), (), s32[]{:S(2)}) async-start(), calls=%async_computation.8 | async-start | bytes 2097152 | tf_op jit(solution)/shard_map/psum | solution.py:95
  223.4 21.5 %collective-permute-start.5 = (bf16[128,3584]{1,0:T(8,128)(2,1)}, bf16[128,3584]{1,0:T(8,128)(2,1)}, u32[]{:S(2)}, u32[]{:S(2)}) collective-permute-start(bf16[128,3584]{1,0:T(8,128)(2,1)} %all_gather.10), channel_id=1, source_target_pairs={{0,8},{8,0},{16,24},{24,16},{1,9},{9,1},{17,25},{25,17},{2,10},{10... | collective-permute-start | bytes 2752520 | tf_op jit(solution)/shard_map/ppermute | solution.py:25
  243.4 21.4 %collective-permute-start.8 = (bf16[128,3584]{1,0:T(8,128)(2,1)S(1)}, bf16[128,3584]{1,0:T(8,128)(2,1)S(1)}, u32[]{:S(2)}, u32[]{:S(2)}) collective-permute-start(bf16[128,3584]{1,0:T(8,128)(2,1)S(1)} %all_gather.11), channel_id=1, source_target_pairs={{0,8},{8,0},{16,24},{24,16},{1,9},{9,1},{17,25},{25,17},{2,10},{10... | collective-permute-start | bytes 2752520 | tf_op jit(solution)/shard_map/ppermute | solution.py:25
  275.8 93.7 %reduce-scatter.11.cloned.1.call-start = ((), (), s32[]{:S(2)}) async-start(), calls=%async_computation.7 | async-start | bytes 1376256 | tf_op jit(solution)/shard_map/reduce_scatter | solution.py:78
  317.1 14.5 %collective-permute-start.6 = (bf16[2048,128]{1,0:T(8,128)(2,1)}, bf16[2048,128]{1,0:T(8,128)(2,1)}, u32[]{:S(2)}, u32[]{:S(2)}) collective-permute-start(bf16[2048,128]{1,0:T(8,128)(2,1)} %reshape.160), channel_id=1, source_target_pairs={{0,8},{8,16},{16,24},{1,9},{9,17},{17,25},{2,10},{10,18},{18,26},{... | collective-permute-start | bytes 1572872 | tf_op jit(solution)/shard_map/ppermute | solution.py:16
  323.5 15.0 %collective-permute-start.7 = (bf16[2048,128]{1,0:T(8,128)(2,1)}, bf16[2048,128]{1,0:T(8,128)(2,1)}, u32[]{:S(2)}, u32[]{:S(2)}) collective-permute-start(bf16[2048,128]{1,0:T(8,128)(2,1)} %reshape.162), channel_id=1, source_target_pairs={{8,0},{16,8},{24,16},{9,1},{17,9},{25,17},{10,2},{18,10},{26,18},{... | collective-permute-start | bytes 1572872 | tf_op jit(solution)/shard_map/ppermute | solution.py:17
Sparse Core Ops, SparseCore 0:
  15.8 21.6 reduce-scatter.4
  83.8 36.3 all-reduce.6
  186.2 17.8 reduce-scatter.6
  206.1 22.9 reduce-scatter.8
  275.9 36.3 all-reduce.4
  351.4 18.0 reduce-scatter.10
where the time goes:
time: 380 us; the launch traced here: 378 us
  waiting for transfers between devices  142 us (37%)
  matrix products  80.9 us (21%)
  local copies, waits for them, and re-layouts  46.4 us (12%)
  blocking collectives  43.9 us (12%)
  other arithmetic  23.8 us (6%)
  starting transfers between devices  21.1 us (6%)
  between operations  20.1 us (5%)
    psum x2, waiting for transfers between devices, shards(): lax.psum(product.astype(jnp.bfloat16), 'row').astype(jnp.float32)  60.3 us
    dot_general x4, matrix products, shards(): lax.dot_general(hid_operand, weight, (((1,), (1,)), ((), ())), preferred_...  44.9 us
    reduce_scatter x4, waiting for transfers between devices, shards(): lax.psum_scatter(feature_term(jnp.int32(0), col_rows * lax.axis_size('col...  44.3 us
    all_gather x3, blocking collectives, shards(): hid_send = lax.all_gather(hid_share, 'col', axis=0, tiled=True)  43.9 us
    dot_general x4, matrix products, feature_term(): return jnp.dot(operand, weight, preferred_element_type=jnp.float32)  33.8 us
    ppermute x3, waiting for transfers between devices, extended_2(): after = lax.ppermute(first, axis, down)  18.2 us
    ppermute x3, waiting for transfers between devices, swapped(): return lax.ppermute(value, axis, pairs)  16.7 us
    ppermute x3, starting transfers between devices, extended_2(): before = lax.ppermute(last, axis, up)  12.1 us
  transfers between devices with their start and end apart: 15, of which 13 were waited for; matrix products, arithmetic and copies ran while one was open for 20% of the time, Pallas kernels for 0%

commit v1 on v0

--- a/solution.py
+++ b/solution.py
@@ -4,6 +4,11 @@
 from jax.sharding import PartitionSpec as P
 
 STEPS = 4
+
+
+def summed_here(value, name):
+    parts = lax.all_gather(value, name)
+    return jnp.sum(parts, axis=0)
 
 
 def extended_2(shard, sides, width):
@@ -92,7 +97,7 @@
         )
         updated = (
             residual.astype(jnp.float32)
-            + lax.psum(product.astype(jnp.bfloat16), "row").astype(jnp.float32)
+            + summed_here(product.astype(jnp.bfloat16), "row").astype(jnp.float32)
         ).astype(jnp.bfloat16)
         fwd_out = jnp.where(is_even, fwd_res, updated)
         bwd_out = jnp.where(is_even, updated, bwd_res)

time: 380 us -> 319 us (0.84)
  local copies, waits for them, and re-layouts: 46.4 us -> 12.7 us
  waiting for transfers between devices: 142 us -> 112 us
  other arithmetic: 23.8 us -> 31.5 us
  blocking collectives: 43.9 us -> 38 us
    psum x2 -> x0, waiting for transfers between devices: 60.3 us -> none  [shards(): lax.psum(product.astype(jnp.bfloat16), 'row').astype(jnp.float32)]
    ppermute x3, waiting for transfers between devices: 16.7 us -> 46.3 us  [swapped(): return lax.ppermute(value, axis, pairs)]
    all_gather x0 -> x4, waiting for transfers between devices: none -> 20.5 us  [summed_here(): parts = lax.all_gather(value, name)]
    reshape x6 -> x0, local copies, waits for them, and re-layouts: 12.5 us -> none  [the longest x3 6.25 us: shards(): fwd_out.reshape(res_rows, 128)]
    ppermute x3, waiting for transfers between devices: 18.2 us -> 6.77 us  [extended_2(): after = lax.ppermute(first, axis, down)]
    reduce_sum x0 -> x4, other arithmetic: none -> 10.9 us  [summed_here(): return jnp.sum(parts, axis=0)]
    reduce_scatter x4, waiting for transfers between devices: 44.3 us -> 36.9 us  [shards(): lax.psum_scatter(feature_term(jnp.int32(0), col_rows * lax.axis_size('col...]
    reshape x3 -> x1, local copies, waits for them, and re-layouts: 6.19 us -> 0.22 us  [shards(): left_resid.reshape(fwd_out.shape)]
  transfers between devices with their start and end apart: 15 -> 17, of which waited for: 13 -> 10; matrix products, arithmetic and copies ran while one was open for 20% -> 22% of each run, Pallas kernels for 0% -> 0%
where the time goes in v1:
time: 319 us; the launch traced here: 318 us
  waiting for transfers between devices  112 us (35%)
  matrix products  80.3 us (25%)
  blocking collectives  38 us (12%)
  other arithmetic  31.5 us (10%)
  starting transfers between devices  21.9 us (7%)
  between operations  21.9 us (7%)
  local copies, waits for them, and re-layouts  12.7 us (4%)
    ppermute x3, waiting for transfers between devices, swapped(): return lax.ppermute(value, axis, pairs)  46.3 us
    dot_general x4, matrix products, shards(): lax.dot_general(hid_operand, weight, (((1,), (1,)), ((), ())), preferred_...  45.3 us
    all_gather x3, blocking collectives, shards(): hid_send = lax.all_gather(hid_share, 'col', axis=0, tiled=True)  38 us
    reduce_scatter x4, waiting for transfers between devices, shards(): lax.psum_scatter(feature_term(jnp.int32(0), col_rows * lax.axis_size('col...  36.9 us
    dot_general x4, matrix products, feature_term(): return jnp.dot(operand, weight, preferred_element_type=jnp.float32)  32.8 us
    all_gather x4, waiting for transfers between devices, summed_here(): parts = lax.all_gather(value, name)  20.5 us
    ppermute x3, starting transfers between devices, extended_2(): before = lax.ppermute(last, axis, up)  12.2 us
    reduce_sum x4, other arithmetic, summed_here(): return jnp.sum(parts, axis=0)  10.9 us
  transfers between devices with their start and end apart: 17, of which 10 were waited for; matrix products, arithmetic and copies ran while one was open for 22% of the time, Pallas kernels for 0%

profile of v1, /device:TPU:0, one launch (start us, length us, event | category | flops | bytes accessed | tf_op | source)
XLA Modules:
  0.0 317.8 jit_solution(7403859451761201332)
XLA Ops:
  8.1 11.5 %fusion.28 = bf16[128,2048]{1,0:T(8,128)(2,1)} fusion(bf16[1,2048,3584]{2,1,0:T(8,128)(2,1)} %param.13, bf16[1,128,3584]{2,1,0:T(8,128)(2,1)} %param.15, bf16[1,128,3584]{2,1,0:T(8,128)(2,1)} %param.17, bf16[4,1,128,3584]{3,2,1,0:T(8,128)(2,1)} %param.18, pred[]{:T(512)S(6)} %eq.66), kind=kOutput, calls=%fused_computation.20 | convolution fusion | flops 1884815360 | bytes 17956864 | tf_op jit(solution)/shard_map/dot_general | solution.py:95
  19.7 8.2 %fusion.16 = bf16[128,3584]{1,0:T(8,128)(2,1)} fusion(bf16[1,2048,3584]{2,1,0:T(8,128)(2,1)} %param.13, bf16[1,128,2048]{2,1,0:T(8,128)(2,1)S(1)} %copy-done.1, bf16[1,128,2048]{2,1,0:T(8,128)(2,1)S(1)} %copy-done.2, pred[]{:T(512)S(6)} %eq.66), kind=kOutput, calls=%fused_computation.16 | convolution fusion | flops 1879769088 | bytes 16646145 | tf_op jit(solution)/shard_map/dot_general | solution.py:81
  38.6 2.1 fusion.145
  43.1 2.2 all-gather.9.cloned.1.call-done
  45.3 2.9 reduce_sum.48
  49.5 2.4 broadcast_select_fusion.10
  51.9 3.5 %collective-permute-start = (bf16[2048,128]{1,0:T(8,128)(2,1)}, bf16[2048,128]{1,0:T(8,128)(2,1)S(1)}, u32[]{:S(2)}, u32[]{:S(2)}) collective-permute-start(bf16[2048,128]{1,0:T(8,128)(2,1)} %get-tuple-element.12), channel_id=1, source_target_pairs={{0,8},{8,16},{16,24},{1,9},{9,17},{17,25},{2,10},{10,18},{18,26},{... | collective-permute-start | bytes 1572872 | tf_op jit(solution)/shard_map/ppermute | solution.py:21
  58.1 13.1 %all_gather.35 = bf16[128,3584]{1,0:T(8,128)(2,1)} all-gather(bf16[64,3584]{1,0:T(8,128)(2,1)S(1)} %fusion.93), channel_id=1, replica_groups=mesh['pipe'=4,'row'=4,'col'=2] {'col'}, dimensions={0}, use_global_device_ids=true | all-gather | bytes 1376256 | tf_op jit(solution)/shard_map/all_gather | solution.py:105
  71.2 2.4 collective-permute-start.2
  74.4 2.1 broadcast_select_fusion.6
  76.7 8.2 %fusion.19 = bf16[128,3584]{1,0:T(8,128)(2,1)} fusion(bf16[128,2048]{1,0:T(8,128)(2,1)S(1)} %select_n.273, bf16[1,2048,3584]{2,1,0:T(8,128)(2,1)} %param.13), kind=kOutput, calls=%fused_computation.17 | convolution fusion | flops 1879506944 | bytes 16121856 | tf_op jit(solution)/shard_map/dot_general | solution.py:81
  85.2 8.0 %collective-permute-done.2 = bf16[128,3584]{1,0:T(8,128)(2,1)} collective-permute-done((bf16[128,3584]{1,0:T(8,128)(2,1)}, bf16[128,3584]{1,0:T(8,128)(2,1)}, u32[]{:S(2)}, u32[]{:S(2)}) %collective-permute-start.2) | collective-permute-done | bytes 917536 | tf_op jit(solution)/shard_map/ppermute | solution.py:30
  93.2 11.7 %fusion.31 = bf16[128,2048]{1,0:T(8,128)(2,1)} fusion(bf16[1,2048,3584]{2,1,0:T(8,128)(2,1)} %param.13, bf16[128,3584]{1,0:T(8,128)(2,1)} %collective-permute-done.2, bf16[4,1,128,3584]{3,2,1,0:T(8,128)(2,1)} %param.18, pred[]{:T(512)S(6)} %eq.66), kind=kOutput, calls=%fused_computation.21 | convolution fusion | flops 1884815360 | bytes 17039360 | tf_op jit(solution)/shard_map/dot_general | solution.py:95
  106.3 11.9 %all_gather.38 = bf16[128,3584]{1,0:T(8,128)(2,1)S(1)} all-gather(bf16[64,3584]{1,0:T(8,128)(2,1)S(1)} %fusion.94), channel_id=1, replica_groups=mesh['pipe'=4,'row'=4,'col'=2] {'col'}, dimensions={0}, use_global_device_ids=true | all-gather | bytes 1376256 | tf_op jit(solution)/shard_map/all_gather | solution.py:105
  119.7 18.8 %collective-permute-done.5 = bf16[128,3584]{1,0:T(8,128)(2,1)S(1)} collective-permute-done((bf16[128,3584]{1,0:T(8,128)(2,1)S(1)}, bf16[128,3584]{1,0:T(8,128)(2,1)S(1)}, u32[]{:S(2)}, u32[]{:S(2)}) %collective-permute-start.5) | collective-permute-done | bytes 917536 | tf_op jit(solution)/shard_map/ppermute | solution.py:30
  138.5 11.0 %fusion.34 = bf16[128,2048]{1,0:T(8,128)(2,1)} fusion(bf16[1,2048,3584]{2,1,0:T(8,128)(2,1)} %param.13, bf16[128,3584]{1,0:T(8,128)(2,1)S(1)} %collective-permute-done.5, bf16[4,1,128,3584]{3,2,1,0:T(8,128)(2,1)} %param.18, pred[]{:T(512)S(6)} %eq.66), kind=kOutput, calls=%fused_computation.22 | convolution fusion | flops 1884815360 | bytes 17039360 | tf_op jit(solution)/shard_map/dot_general | solution.py:95
  149.6 3.0 reduce_sum.49
  155.0 4.0 %collective-permute-start.3 = (bf16[2048,128]{1,0:T(8,128)(2,1)}, bf16[2048,128]{1,0:T(8,128)(2,1)}, u32[]{:S(2)}, u32[]{:S(2)}) collective-permute-start(bf16[2048,128]{1,0:T(8,128)(2,1)} %get-tuple-element.10), channel_id=1, source_target_pairs={{0,8},{8,16},{16,24},{1,9},{9,17},{17,25},{2,10},{10,18},{18,26},{... | collective-permute-start | bytes 1572872 | tf_op jit(solution)/shard_map/ppermute | solution.py:21
  161.7 10.6 %all-gather.13.cloned.1.call-done = bf16[512,2048]{1,0:T(8,128)(2,1)} async-done(((bf16[128,2048]{1,0:T(8,128)(2,1)}), bf16[512,2048]{1,0:T(8,128)(2,1)}) %all-gather.13.cloned.1.call-update) | async-done | bytes 2097168 | tf_op jit(solution)/shard_map/all_gather | solution.py:10
  174.6 2.3 broadcast_select_fusion.5
  177.3 8.2 %fusion.22 = bf16[128,3584]{1,0:T(8,128)(2,1)} fusion(bf16[128,2048]{1,0:T(8,128)(2,1)S(1)} %select_n.283, bf16[1,2048,3584]{2,1,0:T(8,128)(2,1)} %param.13), kind=kOutput, calls=%fused_computation.18 | convolution fusion | flops 1879506944 | bytes 16121856 | tf_op jit(solution)/shard_map/dot_general | solution.py:81
  185.5 19.0 %reduce-scatter.9.cloned.1.call-done = bf16[64,3584]{1,0:T(8,128)(2,1)} async-done(((bf16[128,3584]{1,0:T(8,128)(2,1)}), bf16[64,3584]{1,0:T(8,128)(2,1)}) %reduce-scatter.9.cloned.1.call-update) | async-done | bytes 458768 | tf_op jit(solution)/shard_map/reduce_scatter | solution.py:83
  205.7 12.9 %all_gather.41 = bf16[128,3584]{1,0:T(8,128)(2,1)S(1)} all-gather(bf16[64,3584]{1,0:T(8,128)(2,1)S(1)} %fusion.95), channel_id=1, replica_groups=mesh['pipe'=4,'row'=4,'col'=2] {'col'}, dimensions={0}, use_global_device_ids=true | all-gather | bytes 1376256 | tf_op jit(solution)/shard_map/all_gather | solution.py:105
  220.1 19.5 %collective-permute-done.8 = bf16[128,3584]{1,0:T(8,128)(2,1)S(1)} collective-permute-done((bf16[128,3584]{1,0:T(8,128)(2,1)S(1)}, bf16[128,3584]{1,0:T(8,128)(2,1)S(1)}, u32[]{:S(2)}, u32[]{:S(2)}) %collective-permute-start.8) | collective-permute-done | bytes 917536 | tf_op jit(solution)/shard_map/ppermute | solution.py:30
  239.7 11.0 %fusion.37 = bf16[128,2048]{1,0:T(8,128)(2,1)} fusion(bf16[1,2048,3584]{2,1,0:T(8,128)(2,1)} %param.13, bf16[128,3584]{1,0:T(8,128)(2,1)S(1)} %collective-permute-done.8, bf16[4,1,128,3584]{3,2,1,0:T(8,128)(2,1)} %param.18, pred[]{:T(512)S(6)} %eq.66), kind=kOutput, calls=%fused_computation.23 | convolution fusion | flops 1884815360 | bytes 17039360 | tf_op jit(solution)/shard_map/dot_general | solution.py:95
  252.1 4.6 %collective-permute-start.6 = (bf16[2048,128]{1,0:T(8,128)(2,1)S(1)}, bf16[2048,128]{1,0:T(8,128)(2,1)S(1)}, u32[]{:S(2)}, u32[]{:S(2)}) collective-permute-start(bf16[2048,128]{1,0:T(8,128)(2,1)S(1)} %copy-done.11), channel_id=1, source_target_pairs={{0,8},{8,16},{16,24},{1,9},{9,17},{17,25},{2,10},{10,18},{18,26},{... | collective-permute-start | bytes 1572872 | tf_op jit(solution)/shard_map/ppermute | solution.py:21
  257.6 6.8 %collective-permute-done.7 = bf16[2048,128]{1,0:T(8,128)(2,1)S(1)} collective-permute-done((bf16[2048,128]{1,0:T(8,128)(2,1)S(1)}, bf16[2048,128]{1,0:T(8,128)(2,1)S(1)}, u32[]{:S(2)}, u32[]{:S(2)}) %collective-permute-start.7) | collective-permute-done | bytes 524320 | tf_op jit(solution)/shard_map/ppermute | solution.py:22
  265.8 7.6 %all-gather.15.cloned.1.call-done = bf16[512,2048]{1,0:T(8,128)(2,1)} async-done(((bf16[128,2048]{1,0:T(8,128)(2,1)}), bf16[512,2048]{1,0:T(8,128)(2,1)}) %all-gather.15.cloned.1.call-update) | async-done | bytes 2097168 | tf_op jit(solution)/shard_map/all_gather | solution.py:10
  273.4 2.9 reduce_sum.51
  276.3 2.7 broadcast_select_fusion.12
  281.2 8.3 %fusion.25 = bf16[128,3584]{1,0:T(8,128)(2,1)} fusion(bf16[128,2048]{1,0:T(8,128)(2,1)S(1)} %select_n.292, bf16[1,2048,3584]{2,1,0:T(8,128)(2,1)} %param.13), kind=kOutput, calls=%fused_computation.19 | convolution fusion | flops 1879506944 | bytes 16121856 | tf_op jit(solution)/shard_map/dot_general | solution.py:81
  290.5 17.9 %reduce-scatter.11.cloned.1.call-done = bf16[64,3584]{1,0:T(8,128)(2,1)} async-done(((bf16[128,3584]{1,0:T(8,128)(2,1)}), bf16[64,3584]{1,0:T(8,128)(2,1)}) %reduce-scatter.11.cloned.1.call-update) | async-done | bytes 458768 | tf_op jit(solution)/shard_map/reduce_scatter | solution.py:83
  (100 shorter events, 34.4 us)
Async XLA Ops:
  8.0 34.4 %copy-start = (bf16[8,2048]{1,0:T(8,128)(2,1)S(1)}, bf16[8,2048]{1,0:T(8,128)(2,1)}, u32[]{:S(2)}) copy-start(bf16[8,2048]{1,0:T(8,128)(2,1)} %param.24) | copy-start | bytes 98308
  8.0 37.3 %all-gather.9.cloned.1.call-start = ((), (), s32[]{:S(2)}) async-start(), calls=%async_computation.8 | async-start | bytes 2621440 | tf_op jit(solution)/shard_map/all_gather | solution.py:10
  8.1 11.6 %copy-start.1 = (bf16[1,128,2048]{2,1,0:T(8,128)(2,1)S(1)}, bf16[1,128,2048]{2,1,0:T(8,128)(2,1)}, u32[]{:S(2)}) copy-start(bf16[1,128,2048]{2,1,0:T(8,128)(2,1)} %param.14) | copy-start | bytes 1572868
  8.1 11.6 %copy-start.2 = (bf16[1,128,2048]{2,1,0:T(8,128)(2,1)S(1)}, bf16[1,128,2048]{2,1,0:T(8,128)(2,1)}, u32[]{:S(2)}) copy-start(bf16[1,128,2048]{2,1,0:T(8,128)(2,1)} %param.16) | copy-start | bytes 1572868
  19.6 37.2 %reduce-scatter.5.cloned.1.call-start = ((), (), s32[]{:S(2)}) async-start(), calls=%async_computation.4 | async-start | bytes 1376256 | tf_op jit(solution)/shard_map/reduce_scatter | solution.py:83
  27.9 2.2 copy-start.12
  27.9 8.9 %copy-start.15 = (s32[3,128]{1,0:T(4,128)S(1)}, s32[3,128]{1,0:T(4,128)}, u32[]{:S(2)}) copy-start(s32[3,128]{1,0:T(4,128)} %param.20) | copy-start | bytes 4612
  27.9 77.1 %reduce-scatter.7.cloned.1.call-start = ((), (), s32[]{:S(2)}) async-start(), calls=%async_computation.5 | async-start | bytes 1376256 | tf_op jit(solution)/shard_map/reduce_scatter | solution.py:83
  38.6 3.2 copy-start.13
  38.6 3.8 %copy-start.14 = (bf16[2048]{0:T(1024)(128)(2,1)S(1)}, bf16[2048]{0:T(1024)(128)(2,1)}, u32[]{:S(2)}) copy-start(bf16[2048]{0:T(1024)(128)(2,1)} %param.23) | copy-start | bytes 12292
  51.9 22.4 %copy-start.3 = (bf16[2048,128]{1,0:T(8,128)(2,1)S(1)}, bf16[2048,128]{1,0:T(8,128)(2,1)}, u32[]{:S(2)}) copy-start(bf16[2048,128]{1,0:T(8,128)(2,1)} %squeeze.54) | copy-start | bytes 1572868
  51.9 21.7 %collective-permute-start = (bf16[2048,128]{1,0:T(8,128)(2,1)}, bf16[2048,128]{1,0:T(8,128)(2,1)S(1)}, u32[]{:S(2)}, u32[]{:S(2)}) collective-permute-start(bf16[2048,128]{1,0:T(8,128)(2,1)} %get-tuple-element.12), channel_id=1, source_target_pairs={{0,8},{8,16},{16,24},{1,9},{9,17},{17,25},{2,10},{10,18},{18,26},{... | collective-permute-start | bytes 1572872 | tf_op jit(solution)/shard_map/ppermute | solution.py:21
  55.5 18.1 %collective-permute-start.1 = (bf16[2048,128]{1,0:T(8,128)(2,1)}, bf16[2048,128]{1,0:T(8,128)(2,1)}, u32[]{:S(2)}, u32[]{:S(2)}) collective-permute-start(bf16[2048,128]{1,0:T(8,128)(2,1)} %get-tuple-element.13), channel_id=1, source_target_pairs={{8,0},{16,8},{24,16},{9,1},{17,9},{25,17},{10,2},{18,10},{26,18},{... | collective-permute-start | bytes 1572872 | tf_op jit(solution)/shard_map/ppermute | solution.py:22
  71.2 22.0 %collective-permute-start.2 = (bf16[128,3584]{1,0:T(8,128)(2,1)}, bf16[128,3584]{1,0:T(8,128)(2,1)}, u32[]{:S(2)}, u32[]{:S(2)}) collective-permute-start(bf16[128,3584]{1,0:T(8,128)(2,1)} %all_gather.35), channel_id=1, source_target_pairs={{0,8},{8,0},{16,24},{24,16},{1,9},{9,1},{17,25},{25,17},{2,10},{10... | collective-permute-start | bytes 2752520 | tf_op jit(solution)/shard_map/ppermute | solution.py:30
  84.9 64.6 %all-gather.11.cloned.1.call-start = ((), (), s32[]{:S(2)}) async-start(), calls=%async_computation.9 | async-start | bytes 2621440 | tf_op jit(solution)/shard_map/all_gather | solution.py:10
  104.9 67.4 %all-gather.13.cloned.1.call-start = ((), (), s32[]{:S(2)}) async-start(), calls=%async_computation.10 | async-start | bytes 2621440 | tf_op jit(solution)/shard_map/all_gather | solution.py:10
  118.2 20.2 %collective-permute-start.5 = (bf16[128,3584]{1,0:T(8,128)(2,1)S(1)}, bf16[128,3584]{1,0:T(8,128)(2,1)S(1)}, u32[]{:S(2)}, u32[]{:S(2)}) collective-permute-start(bf16[128,3584]{1,0:T(8,128)(2,1)S(1)} %all_gather.38), channel_id=1, source_target_pairs={{0,8},{8,0},{16,24},{24,16},{1,9},{9,1},{17,25},{25,17},{2,10},{10... | collective-permute-start | bytes 2752520 | tf_op jit(solution)/shard_map/ppermute | solution.py:30
  149.5 54.9 %reduce-scatter.9.cloned.1.call-start = ((), (), s32[]{:S(2)}) async-start(), calls=%async_computation.6 | async-start | bytes 1376256 | tf_op jit(solution)/shard_map/reduce_scatter | solution.py:83
  149.6 4.3 %copy-start.4 = (bf16[2048,128]{1,0:T(8,128)(2,1)S(1)}, bf16[2048,128]{1,0:T(8,128)(2,1)}, u32[]{:S(2)}) copy-start(bf16[2048,128]{1,0:T(8,128)(2,1)} %get-tuple-element.6) | copy-start | bytes 1572868
  149.6 4.3 %copy-start.5 = (bf16[2048,128]{1,0:T(8,128)(2,1)S(1)}, bf16[2048,128]{1,0:T(8,128)(2,1)}, u32[]{:S(2)}) copy-start(bf16[2048,128]{1,0:T(8,128)(2,1)} %get-tuple-element.7) | copy-start | bytes 1572868
  155.0 5.7 %copy-start.7 = (bf16[1,128,2048]{2,1,0:T(8,128)(2,1)S(1)}, bf16[1,128,2048]{2,1,0:T(8,128)(2,1)}, u32[]{:S(2)}) copy-start(bf16[1,128,2048]{2,1,0:T(8,128)(2,1)} %get-tuple-element.18) | copy-start | bytes 1572868
  155.0 19.6 %collective-permute-start.3 = (bf16[2048,128]{1,0:T(8,128)(2,1)}, bf16[2048,128]{1,0:T(8,128)(2,1)}, u32[]{:S(2)}, u32[]{:S(2)}) collective-permute-start(bf16[2048,128]{1,0:T(8,128)(2,1)} %get-tuple-element.10), channel_id=1, source_target_pairs={{0,8},{8,16},{16,24},{1,9},{9,17},{17,25},{2,10},{10,18},{18,26},{... | collective-permute-start | bytes 1572872 | tf_op jit(solution)/shard_map/ppermute | solution.py:21
  159.1 15.5 %collective-permute-start.4 = (bf16[2048,128]{1,0:T(8,128)(2,1)}, bf16[2048,128]{1,0:T(8,128)(2,1)}, u32[]{:S(2)}, u32[]{:S(2)}) collective-permute-start(bf16[2048,128]{1,0:T(8,128)(2,1)} %get-tuple-element.11), channel_id=1, source_target_pairs={{8,0},{16,8},{24,16},{9,1},{17,9},{25,17},{10,2},{18,10},{26,18},{... | collective-permute-start | bytes 1572872 | tf_op jit(solution)/shard_map/ppermute | solution.py:22
  185.5 88.0 %all-gather.15.cloned.1.call-start = ((), (), s32[]{:S(2)}) async-start(), calls=%async_computation.11 | async-start | bytes 2621440 | tf_op jit(solution)/shard_map/all_gather | solution.py:10
  218.7 33.4 %copy-start.11 = (bf16[2048,128]{1,0:T(8,128)(2,1)S(1)}, bf16[2048,128]{1,0:T(8,128)(2,1)}, u32[]{:S(2)}) copy-start(bf16[2048,128]{1,0:T(8,128)(2,1)} %get-tuple-element.2) | copy-start | bytes 1572868
  218.7 21.0 %collective-permute-start.8 = (bf16[128,3584]{1,0:T(8,128)(2,1)S(1)}, bf16[128,3584]{1,0:T(8,128)(2,1)S(1)}, u32[]{:S(2)}, u32[]{:S(2)}) collective-permute-start(bf16[128,3584]{1,0:T(8,128)(2,1)S(1)} %all_gather.41), channel_id=1, source_target_pairs={{0,8},{8,0},{16,24},{24,16},{1,9},{9,1},{17,25},{25,17},{2,10},{10... | collective-permute-start | bytes 2752520 | tf_op jit(solution)/shard_map/ppermute | solution.py:30
  250.7 57.7 %reduce-scatter.11.cloned.1.call-start = ((), (), s32[]{:S(2)}) async-start(), calls=%async_computation.7 | async-start | bytes 1376256 | tf_op jit(solution)/shard_map/reduce_scatter | solution.py:83
  250.8 13.6 %collective-permute-start.7 = (bf16[2048,128]{1,0:T(8,128)(2,1)S(1)}, bf16[2048,128]{1,0:T(8,128)(2,1)S(1)}, u32[]{:S(2)}, u32[]{:S(2)}) collective-permute-start(bf16[2048,128]{1,0:T(8,128)(2,1)S(1)} %get-tuple-element.20), channel_id=1, source_target_pairs={{8,0},{16,8},{24,16},{9,1},{17,9},{25,17},{10,2},{18,10},{26,18},{... | collective-permute-start | bytes 1572872 | tf_op jit(solution)/shard_map/ppermute | solution.py:22
  252.1 13.5 %collective-permute-start.6 = (bf16[2048,128]{1,0:T(8,128)(2,1)S(1)}, bf16[2048,128]{1,0:T(8,128)(2,1)S(1)}, u32[]{:S(2)}, u32[]{:S(2)}) collective-permute-start(bf16[2048,128]{1,0:T(8,128)(2,1)S(1)} %copy-done.11), channel_id=1, source_target_pairs={{0,8},{8,16},{16,24},{1,9},{9,17},{17,25},{2,10},{10,18},{18,26},{... | collective-permute-start | bytes 1572872 | tf_op jit(solution)/shard_map/ppermute | solution.py:21
  264.4 11.9 %copy-start.8 = (bf16[2048,128]{1,0:T(8,128)(2,1)}, bf16[2048,128]{1,0:T(8,128)(2,1)S(1)}, u32[]{:S(2)}) copy-start(bf16[2048,128]{1,0:T(8,128)(2,1)S(1)} %collective-permute-done.7) | copy-start | bytes 1572868
  265.6 10.8 %copy-start.9 = (bf16[2048,128]{1,0:T(8,128)(2,1)}, bf16[2048,128]{1,0:T(8,128)(2,1)S(1)}, u32[]{:S(2)}) copy-start(bf16[2048,128]{1,0:T(8,128)(2,1)S(1)} %collective-permute-done.6) | copy-start | bytes 1572868
  281.1 8.3 %copy-start.6 = (bf16[1,128,2048]{2,1,0:T(8,128)(2,1)S(1)}, bf16[1,128,2048]{2,1,0:T(8,128)(2,1)}, u32[]{:S(2)}) copy-start(bf16[1,128,2048]{2,1,0:T(8,128)(2,1)} %get-tuple-element.9) | copy-start | bytes 1572868
  (1 other events, 0.8 us)
Sparse Core Ops, SparseCore 0:
  19.7 25.5 all-gather.8
  105.1 23.6 all-gather.10
  149.6 22.6 all-gather.12
  250.8 22.5 all-gather.14
Sparse Core Ops, SparseCore 1:
  28.0 21.9 reduce-scatter.4
  85.0 19.2 reduce-scatter.6
  185.5 18.9 reduce-scatter.8
  289.5 18.8 reduce-scatter.10
